TPU v7x, 32 devices: a whole 2x2x4 slice. The times are simulated.
32 devices in a mesh: shard: 4 (over x, core), context: 4 (over z), tensor: 2 (over y).
Axes of the slice: x: 2, y: 2, z: 4, core: 2. Of those that a mesh axis runs over, the one named last changes fastest.
Arguments:
- hidden_in: bfloat16 [2048, 1536], P(('shard', 'context')), may hold values from -6 to 6
- segment_ids: int32 [4, 512], P('shard'), may hold values from 0 to 2, never falling along the last dimension, each value on 1 to 256 neighbouring positions
- attn_gain: bfloat16 [1536], P(('shard', 'context')), may hold values from 0.25 to 1.75
- qkv_weight: bfloat16 [1536, 2048], P(('shard', 'context'), 'tensor'), may hold values from -0.15625 to 0.15625
- qkv_bias: bfloat16 [16, 128], P('tensor', ('shard', 'context')), may hold values from -3 to 3
- out_weight: bfloat16 [1536, 1536], P('tensor', ('shard', 'context')), may hold values from -0.625 to 0.625
- ffn_gain: bfloat16 [1536], P(('shard', 'context')), may hold values from 0.25 to 1.75
- gate_weight: bfloat16 [1536, 8960], P(('shard', 'context'), 'tensor'), may hold values from -0.15625 to 0.15625
- up_weight: bfloat16 [1536, 8960], P(('shard', 'context'), 'tensor'), may hold values from -0.15625 to 0.15625
- down_weight: bfloat16 [8960, 1536], P('tensor', ('shard', 'context')), may hold values from -0.0625 to 0.0625
- out_cotangent: bfloat16 [2048, 1536], P(('shard', 'context')), may hold values from -6 to 6
Outputs:
- block_out: bfloat16 [2048, 1536], P(('shard', 'context'))
- input_grad: float32 [2048, 1536], P(('shard', 'context'))
- attn_gain_grad: float32 [1536], P(('shard', 'context'))
- qkv_weight_grad: float32 [1536, 2048], P(('shard', 'context'), 'tensor')
- qkv_bias_grad: float32 [16, 128], P('tensor', ('shard', 'context'))
- out_weight_grad: float32 [1536, 1536], P('tensor', ('shard', 'context'))
- ffn_gain_grad: float32 [1536], P(('shard', 'context'))
- gate_weight_grad: float32 [1536, 8960], P(('shard', 'context'), 'tensor')
- up_weight_grad: float32 [1536, 8960], P(('shard', 'context'), 'tensor')
- down_weight_grad: float32 [8960, 1536], P('tensor', ('shard', 'context'))
Inputs may be any that keep to these rules, and one draw needn't show every extreme that they name: `segment_ids`: in every group the sequence numbers start at 0 and never fall; a sequence has at most 256 tokens, and one sequence of each group has exactly 256.
All inputs are finite; a program needn't handle non-finite values.
Results may differ from a plain program's by a relative error of at most 0.018.
Values may be sent and summed in bfloat16 or wider, within the bound.
A program may use at most 256 MiB of HBM per device.

v0:
```python
import functools
import math

import jax
import jax.numpy as jnp
from jax import lax
from jax.experimental import pallas as pl
from jax.experimental.pallas import tpu as pltpu
from jax.sharding import PartitionSpec as P

H = 12
KVH = 2
HD = 128
LANES = 128
SUBLANES = 16
BF16 = jnp.bfloat16
F32 = jnp.float32

EPSILON = 1e-06
THETA = 1000000.0

OWNERS = ("shard", "context")
TEAM = ("context", "tensor")
MESH = pl.DeviceIdType.MESH
VMEM_BYTES = 62 * 1024 * 1024


def dot(left, right):
    return jnp.dot(left, right, preferred_element_type=F32)


def contract_last(left, right):
    return lax.dot_general(left, right, (((1,), (1,)), ((), ())), preferred_element_type=F32)


def contract_first(left, right):
    return lax.dot_general(left, right, (((0,), (0,)), ((), ())), preferred_element_type=F32)


def batched(left, right, left_dim, right_dim):
    return lax.dot_general(
        left, right, (((left_dim,), (right_dim,)), ((0,), (0,))), preferred_element_type=F32
    )


def norm_forward(values, gain):
    factor = lax.rsqrt(jnp.mean(values * values, axis=1, keepdims=True) + EPSILON)
    unit = values * factor
    return ((unit * gain).astype(BF16), unit, factor)


def norm_backward(grad_out, unit, factor, gain):
    gain_grad = jnp.sum(grad_out * unit, axis=0)
    scaled = grad_out * gain
    return (gain_grad, factor * (scaled - unit * jnp.mean(scaled * unit, axis=1, keepdims=True)))


def rotary_tables(positions):
    half = HD // 2
    freqs = THETA ** (-(2.0 * jnp.arange(half, dtype=F32)) / HD)
    angles = positions.astype(F32)[:, None] * freqs[None, :]
    cosine, sine = jnp.cos(angles), jnp.sin(angles)
    return (
        jnp.concatenate([cosine, cosine], axis=1),
        jnp.concatenate([-sine, sine], axis=1),
    )


def swap_halves(values):
    half = values.shape[-1] // 2
    return jnp.concatenate([values[..., half:], values[..., :half]], axis=-1)


def rotate(values, cosine, sine):
    return values * cosine + swap_halves(values) * sine


def unrotate(values, cosine, sine):
    return values * cosine - swap_halves(values) * sine


class Place:
    def __init__(self, ns, nz):
        self.ns, self.nz, self.no = ns, nz, ns // 2
        self.s, self.z, self.y = (lax.axis_index(a) for a in ("shard", "context", "tensor"))
        self.core = lax.rem(self.s, 2)
        self.outer = lax.div(self.s, 2)
        self.mate = self.s + 1 - 2 * self.core
        self.twin = 1 - self.y

    def z_to(self, d):
        return lax.rem(self.z + d, self.nz)

    def z_from(self, d):
        return lax.rem(self.z - d + self.nz, self.nz)

    def near(self):
        for k in range(1, self.nz):
            yield (self.z + k < self.nz, lax.rem(self.z + k, self.nz))
            yield (self.z >= k, lax.rem(self.z - k + self.nz, self.nz))

    def s_to(self, o):
        return lax.rem(self.outer + o, self.no) * 2 + self.core

    def s_from(self, o):
        return lax.rem(self.outer - o + self.no, self.no) * 2 + self.core

    def mate_from(self, o):
        return lax.rem(self.outer - o + self.no, self.no) * 2 + 1 - self.core

    def mate_to(self, o):
        return lax.rem(self.outer + o, self.no) * 2 + 1 - self.core

    def greet(self, everyone=False):
        barrier = pltpu.get_barrier_semaphore()
        peers = [{"context": self.z_to(d)} for d in range(1, self.nz)]
        if everyone:
            peers += [{"shard": lax.rem(self.s + k, self.ns)} for k in range(1, self.ns)]
        else:
            peers += [{"shard": self.s_to(o)} for o in range(1, self.no)] + [{"shard": self.mate}]
        peers += [{"tensor": self.twin}]
        for peer in peers:
            pl.semaphore_signal(barrier, inc=1, device_id=peer, device_id_type=MESH)
        pl.semaphore_wait(barrier, len(peers))


class Sends:
    def __init__(self):
        self.remote, self.local = [], []

    def go(self, src, dst, send, recv, only=None, **peer):
        copy = pltpu.make_async_remote_copy(
            src_ref=src, dst_ref=dst, send_sem=send, recv_sem=recv,
            device_id=peer, device_id_type=MESH,
        )
        guarded(only, copy.start)
        self.remote.append((only, copy.wait_send))

    def here(self, src, dst, sem):
        copy = pltpu.make_async_copy(src, dst, sem)
        copy.start()
        self.local.append(copy)

    def drain(self):
        for only, wait in self.remote:
            guarded(only, wait)
        for copy in self.local:
            copy.wait()
        self.remote, self.local = [], []


def both(one, other):
    return other if one is None else one & other


def guarded(only, action):
    if only is None:
        action()
    else:
        pl.when(only)(action)


def landed(ref, send, recv, only=None, **peer):
    copy = pltpu.make_async_remote_copy(
        src_ref=ref, dst_ref=ref, send_sem=send, recv_sem=recv,
        device_id=peer, device_id_type=MESH,
    )
    guarded(only, copy.wait_recv)


def far_first(n):
    return [n - 1 - i // 2 if i % 2 == 0 else i // 2 for i in range(n)]


class Chain:
    def __init__(self, at, sends, ref, sems):
        self.at, self.sends, self.ref = at, sends, ref
        self.zs, self.zr = sems

    @staticmethod
    def sems(nz):
        dma = pltpu.SemaphoreType.DMA
        return [dma((2, nz)), dma((nz,))]

    def hops(self, steps=None):
        at = self.at
        for k in steps or range(1, at.nz):
            yield (-1, at.z - k >= 0, at.z - k)
            yield (1, at.z + k < at.nz, at.z + k)

    def hand(self, way, origin, src, only):
        at = self.at
        there = at.z + 1 < at.nz if way == 0 else at.z > 0
        self.sends.go(
            src, self.ref(origin), self.zs.at[way, origin], self.zr.at[origin],
            only=there if only is None else there & only, context=at.z + (1 if way == 0 else -1),
        )

    def begin(self, src):
        for way in range(2):
            self.hand(way, self.at.z, src, None)

    def step(self, side, valid, origin):
        ref = self.ref(origin)
        landed(ref, self.zs.at[0, origin], self.zr.at[origin], only=valid, context=self.at.z)
        self.hand(0 if side < 0 else 1, origin, ref, valid)
        return ref


class ChainSum:
    def __init__(self, at, sends, bufs, sems):
        self.at, self.sends = at, sends
        stage, self.land = bufs
        self.stage = stage if callable(stage) else lambda z2: stage.at[z2]
        self.zs, self.zr = sems

    @staticmethod
    def sems(nz):
        dma = pltpu.SemaphoreType.DMA
        return [dma((nz,)), dma((nz + 1,))]

    @staticmethod
    def bufs(nz, shape, dtype=BF16):
        return [pltpu.VMEM((nz, *shape), dtype), pltpu.VMEM((nz + 1, *shape), dtype)]

    def put(self, z2, own):
        at = self.at
        stage, dtype = self.stage(z2), self.land.dtype

        def start(slot, before):
            slot_ref = self.land.at[z2]

            @pl.when(before)
            def _():
                landed(slot_ref, self.zs.at[z2], self.zr.at[z2], context=at.z)
                stage[...] = (own() + self.land[z2].astype(F32)).astype(dtype)

            @pl.when(jnp.logical_not(before))
            def _():
                stage[...] = own().astype(dtype)

            pltpu.make_async_remote_copy(
                src_ref=stage, dst_ref=self.land.at[slot], send_sem=self.zs.at[z2],
                recv_sem=self.zr.at[slot], device_id={"context": at.z + (1 if z2_right else -1)},
                device_id_type=MESH,
            ).start()

        for z2_right in (True, False):
            away = at.z < z2 if z2_right else at.z > z2

            @pl.when(away)
            def _(z2_right=z2_right):
                near = at.z + 1 == z2 if z2_right else at.z - 1 == z2
                slot = z2 if z2_right else z2 + near * (at.nz - z2)
                before = at.z > 0 if z2_right else at.z + 1 < at.nz
                start(slot, before)

        self.sends.remote.append((
            at.z != z2,
            lambda: pltpu.make_async_remote_copy(
                src_ref=stage, dst_ref=self.land.at[z2], send_sem=self.zs.at[z2],
                recv_sem=self.zr.at[z2], device_id={"context": at.z}, device_id_type=MESH,
            ).wait_send(),
        ))

    def total(self, own):
        at = self.at
        total = own
        for slot, there in ((at.z, at.z > 0), (at.nz, at.z + 1 < at.nz)):
            landed(self.land.at[slot], self.zs.at[0], self.zr.at[slot], only=there, context=at.z)
            total = total + jnp.where(there, self.land[slot].astype(F32), 0.0)
        return total


class Spread:
    def __init__(self, at, sends, src, dst, sems, same=False):
        self.at, self.sends, self.src, self.dst = at, sends, src, dst
        self.copy = None
        self.own, self.zs, self.zr, self.xs, self.xr, self.cs, self.cr, *chain = sems
        self.chain = Chain(at, sends, lambda z1: dst(at.s, z1), chain) if same else None

    @staticmethod
    def sems(ns, nz):
        dma, no = pltpu.SemaphoreType.DMA, ns // 2
        return [
            dma, dma((nz,)), dma((nz,)), dma((nz, no)), dma((nz, no)), dma((no, nz)), dma((no, nz)),
        ] + Chain.sems(nz)

    def over_z(self):
        at = self.at
        if self.chain is not None:
            self.chain.begin(self.src(at.z))
            return
        for there, z2 in at.near():
            self.sends.go(
                self.src(z2), self.dst(at.s, at.z), self.zs.at[z2], self.zr.at[at.z], only=there,
                context=z2,
            )

    def over_s(self, z1, ref, only=None):
        at = self.at
        for o in range(1, at.no):
            self.sends.go(
                ref, self.dst(at.s, z1), self.xs.at[z1, o], self.xr.at[z1, o], only=only,
                shard=at.s_to(o),
            )
        self.sends.go(
            ref, self.dst(at.s, z1), self.cs.at[0, z1], self.cr.at[0, z1], only=only, shard=at.mate
        )

    def own_block(self):
        at = self.at
        self.over_s(at.z, self.src(at.z))
        self.copy = pltpu.make_async_copy(self.src(at.z), self.dst(at.s, at.z), self.own)
        self.copy.start()

    def pass_z(self, steps=None):
        at = self.at
        if self.chain is not None:
            for side, valid, z1 in self.chain.hops(steps):
                self.over_s(z1, self.chain.step(side, valid, z1), only=valid)
            return
        for there, z1 in at.near():
            ref = self.dst(at.s, z1)
            landed(ref, self.zs.at[z1], self.zr.at[z1], only=there, context=z1)
            self.over_s(z1, ref, only=there)

    def pass_s(self):
        at = self.at
        for o in range(1, at.no):
            s1 = at.s_from(o)
            for d in range(at.nz):
                z1 = at.z_from(d)
                ref = self.dst(s1, z1)
                landed(ref, self.xs.at[z1, o], self.xr.at[z1, o], shard=s1)
                self.sends.go(ref, ref, self.cs.at[o, z1], self.cr.at[o, z1], shard=at.mate)

    def finish(self):
        at = self.at
        self.copy.wait()
        for o in range(at.no):
            for z1 in range(at.nz):
                ref = self.dst(at.mate_from(o), z1)
                landed(ref, self.cs.at[o, z1], self.cr.at[o, z1], shard=at.mate)

    def pass_all(self):
        self.pass_z()
        self.pass_s()


class Tokens:
    def __init__(self, at, sends, ref, sems):
        self.at, self.sends, self.ref = at, sends, ref
        self.ys, self.yr, *chain = sems
        self.chain = Chain(at, sends, lambda z1: ref.at[z1, at.y], chain)

    @staticmethod
    def sems(nz):
        dma = pltpu.SemaphoreType.DMA
        return [dma((nz,)), dma((nz,))] + Chain.sems(nz)

    def over_z(self, src):
        self.chain.begin(src)

    def over_y(self, z1, src, only=None):
        at = self.at
        self.sends.go(
            src, self.ref.at[z1, at.y], self.ys.at[z1], self.yr.at[z1], only=only, tensor=at.twin
        )

    def pass_z(self, steps=None):
        for side, valid, z1 in self.chain.hops(steps):
            self.over_y(z1, self.chain.step(side, valid, z1), only=valid)

    def wait_y(self, places, only=None):
        at = self.at
        for z1 in places:
            ref = self.ref.at[z1, at.twin]
            landed(
                ref, self.ys.at[z1], self.yr.at[z1], only=only and only(z1), tensor=at.twin
            )


def whole_lines(small, blocks, depth):
    tiles = []
    for t in range(blocks * depth // LANES):
        tile = jnp.zeros((8, LANES), F32)
        lane = lax.broadcasted_iota(jnp.int32, (8, LANES), 1) + t * LANES
        for b in range(t * LANES // depth, min(blocks, -(-(t + 1) * LANES // depth))):
            line = small[b, :8, :].astype(F32)
            shift = (b * depth - t * LANES) % LANES
            moved = pltpu.roll(line, shift, 1) if shift else line
            tile = jnp.where((lane >= b * depth) & (lane < (b + 1) * depth), moved, tile)
        tiles.append(tile)
    return jnp.concatenate(tiles, axis=1)


def turn_first(left, right):
    return lax.dot_general(left, right, (((0,), (0,)), ((), ())), preferred_element_type=F32)


def turn_last(left, right):
    return lax.dot_general(left, right, (((1,), (1,)), ((), ())), preferred_element_type=F32)


class Return:
    def __init__(self, at, sends, make, room, lands, out, sems):
        self.at, self.sends, self.make, self.out = at, sends, make, out
        self.stage, self.acc = room.at[pl.ds(0, at.no)], room.at[pl.ds(at.no, at.no)]
        self.landc, self.landx = lands
        self.cs, self.cr, self.xs, self.xr, self.zs, self.zr, self.own = sems
        self.chain, self.short = None, 0
        self.depth = self.acc.shape[1] // at.nz

    @staticmethod
    def sems(ns, nz):
        dma, no = pltpu.SemaphoreType.DMA, ns // 2
        return [
            dma((no,)), dma((no,)), dma((no, nz)), dma((no, nz)), dma((2, nz)), dma((2, nz)), dma((2,)),
        ]

    @staticmethod
    def lands(ns, nz, depth, cols):
        no = ns // 2
        return [pltpu.VMEM((n, nz * depth, cols), BF16) for n in (no, no - 1)]

    def to_mate(self, o):
        return pltpu.make_async_remote_copy(
            src_ref=self.stage.at[o], dst_ref=self.landc.at[o], send_sem=self.cs.at[o],
            recv_sem=self.cr.at[o], device_id={"shard": self.at.mate}, device_id_type=MESH,
        )

    def give_all(self):
        at = self.at

        @pl.loop(0, at.no)
        def _(i):
            o = at.no - 1 - i
            self.stage[o] = self.make(at.mate_to(o)).astype(BF16)
            self.to_mate(o).start()
            self.acc[o] = self.make(at.s_to(o)).astype(BF16)

        self.sends.remote += [(None, self.to_mate(o).wait_send) for o in range(at.no)]

    def rows(self, z2):
        start = z2 * self.depth
        start = start if isinstance(start, int) else pl.multiple_of(start, SUBLANES)
        return pl.ds(start, self.depth)

    def piece(self, z2):
        return self.acc.at[0, self.rows(z2)]

    def slots(self):
        if self.chain is not None:
            return [(None, z2) for z2 in far_first(self.at.nz)]
        return [*self.at.near(), (None, self.at.z)]

    def add(self, o, z2, others):
        line = self.rows(z2)
        total = self.acc[o, line, :].astype(F32)
        for other, k in others:
            total = total + other[k, line, :].astype(F32)
        self.acc[o, line, :] = total.astype(BF16)

    def over_s(self, first=True, last=True):
        at = self.at
        slots = self.slots()
        middle = len(slots) // 2
        slots = (slots[:middle] if first else []) + (slots[middle:] if last else [])
        for o in range(1, at.no):
            if first:
                landed(self.landc.at[o], self.cs.at[o], self.cr.at[o], shard=at.mate)
            for there, z2 in slots:
                line = self.rows(z2)
                guarded(there, lambda: self.add(o, z2, [(self.landc, o)]))
                self.sends.go(
                    self.acc.at[o, line], self.landx.at[o - 1, line], self.xs.at[o, z2],
                    self.xr.at[o, z2], only=there, shard=at.s_to(o),
                )
        if first:
            landed(self.landc.at[0], self.cs.at[0], self.cr.at[0], shard=at.mate)

    def over_z(self, first=True, last=True):
        at = self.at
        slots = self.slots()
        middle = len(slots) // 2
        slots = (slots[:middle] if first else []) + (slots[middle:] if last else [])
        for there, z2 in slots:
            line = self.rows(z2)
            for o in range(1, at.no):
                landed(
                    self.landx.at[o - 1, line], self.xs.at[o, z2], self.xr.at[o, z2], only=there,
                    shard=at.s_from(o),
                )
            terms = [(self.landc, 0)] + [(self.landx, o - 1) for o in range(1, at.no)]
            guarded(there, lambda: self.add(0, z2, terms))
            if self.chain is not None:
                self.chain.put(z2, lambda: self.piece(z2)[...].astype(F32))
                continue
            for w, (cols, whole) in enumerate(self.wings(at.z)):
                src, dst = self.piece(z2).at[:, cols], self.out(at.z, cols)
                if there is not None:
                    self.sends.go(
                        src, dst, self.zs.at[w, z2], self.zr.at[w, at.z], only=both(whole, there),
                        context=z2,
                    )
                else:
                    copy = pltpu.make_async_copy(src, dst, self.own.at[w])
                    guarded(whole, copy.start)

    def wings(self, z1):
        unit, short = self.acc.shape[2], self.short
        yield (pl.ds(0, unit - short), None)
        if short:
            yield (pl.ds(unit - short, short), z1 + 1 < self.at.nz)

    def finish(self):
        at = self.at
        for w, (cols, whole) in enumerate(self.wings(at.z)):
            copy = pltpu.make_async_copy(
                self.piece(at.z).at[:, cols], self.out(at.z, cols), self.own.at[w]
            )
            guarded(whole, copy.wait)
        for there, z1 in at.near():
            for w, (cols, whole) in enumerate(self.wings(z1)):
                landed(
                    self.out(z1, cols), self.zs.at[w, z1], self.zr.at[w, z1],
                    only=both(whole, there), context=z1,
                )


class Reduce:
    def __init__(self, at, sends, parts, bufs, sems):
        self.at, self.sends, self.parts = at, sends, parts
        self.landy, *chain = bufs
        self.ys, self.yr, *chain_sems = sems
        self.chain = ChainSum(at, sends, chain, chain_sems)

    @staticmethod
    def sems(nz):
        dma = pltpu.SemaphoreType.DMA
        return [dma((nz,)), dma((nz,))] + ChainSum.sems(nz)

    @staticmethod
    def bufs(nz, half, width):
        return [pltpu.VMEM((nz, half, width), BF16)] + ChainSum.bufs(nz, (half, width))

    def over_y(self, places):
        at = self.at
        for z2 in places:
            self.sends.go(
                self.parts.at[z2, at.twin], self.landy.at[z2], self.ys.at[z2], self.yr.at[z2],
                tensor=at.twin,
            )

    def own(self, z2):
        return self.parts[z2, self.at.y].astype(F32) + self.landy[z2].astype(F32)

    def pass_y(self, places):
        at = self.at
        for z2 in places:
            landed(self.landy.at[z2], self.ys.at[z2], self.yr.at[z2], tensor=at.twin)
            self.chain.put(z2, lambda z2=z2: self.own(z2))

    def total(self):
        return self.chain.total(self.own(self.at.z))


def piece_of_lines(lines, b, depth):
    first, off = divmod(b * depth, LANES)
    tile = lines[:, first * LANES:(first + 1) * LANES]
    if not off:
        return tile
    tile = pltpu.roll(tile, LANES - off, 1)
    if off + depth <= LANES:
        return tile
    after = pltpu.roll(lines[:, (first + 1) * LANES:(first + 2) * LANES], LANES - off, 1)
    lane = lax.broadcasted_iota(jnp.int32, (8, LANES), 1)
    return jnp.where(lane < LANES - off, tile, after)


class Refs:
    def __init__(self, refs):
        self.refs, self.next = refs, 0

    def take(self, n):
        self.next += n
        return self.refs[self.next - n:self.next]


def layer_kernel(ns, nz, heads, kv, *refs):
    refs = Refs(refs)
    (qkv_in, out_in, small_in, gate_in, up_in, down_in, hidden, cot_in, segments) = refs.take(9)
    (block_out, input_grad, qkv_grad, out_grad, small_out, *ffn_out) = refs.take(8)
    at = Place(ns, nz)
    w_sends, sends = Sends(), Sends()
    depth = qkv_in.shape[0]
    rows, width = hidden.shape
    half = rows // 2
    group_rows = nz * rows
    q_cols = heads * HD
    qkv_cols = q_cols + 2 * kv * HD
    wide = nz * depth
    scale = HD ** (-0.5)
    repeat = heads // kv

    wa, gate_w, up_w, down_w = refs.take(4)
    n_spread, n_tokens, n_ret = len(Spread.sems(ns, nz)), len(Tokens.sems(nz)), len(Return.sems(ns, nz))
    n_red, n_sum = len(Reduce.sems(nz)), len(ChainSum.sems(nz))
    (small, ypart, yland, n2, cot, resid, query, kv_all, probs, attn) = refs.take(10)

    def block(ref):
        return lambda s1, z1: ref.at[s1, pl.ds(pl.multiple_of(z1 * depth, SUBLANES), depth)]

    w_qkv, w_out = (
        Spread(at, w_sends, lambda z2, src=src: src, block(dst), refs.take(n_spread), True)
        for src, dst in (
            (qkv_in, wa.at[:, :, pl.ds(0, qkv_cols)]), (out_in, wa.at[:, :, pl.ds(qkv_cols, q_cols)]),
        )
    )
    w_small = Spread(
        at, w_sends, lambda z2: small_in, lambda s1, z1: small.at[s1 * nz + z1],
        refs.take(n_spread), True,
    )
    ffn = [
        Spread(at, w_sends, lambda z2, src=src: src.at[z2], block(dst), refs.take(n_spread))
        for src, dst in ((gate_in, gate_w), (up_in, up_w), (down_in, down_w))
    ]
    t_cot = Tokens(at, sends, cot, refs.take(n_tokens))
    t_n2 = Tokens(at, sends, n2, refs.take(n_tokens))
    kvs, kvr, yps, ypr, cot_sem = refs.take(5)
    gate, up_val, d_act, act, d_gate, d_up, ffn_part, dn2_part = refs.take(8)
    normed1_b, d_resid_b, d_projb = refs.take(3)

    def columns(ref, s1):
        return ref[..., pl.ds(pl.multiple_of(s1 * wide, LANES), wide)].reshape(-1, wide)

    unit = gate_w.shape[2]

    def out_place(ref):
        return lambda z1, cols: ref.at[
            :, pl.ds(pl.multiple_of(z1 * unit + cols.start, LANES), cols.size)
        ]

    makers = (
        lambda s1: turn_first(columns(n2, s1), d_gate[...]),
        lambda s1: turn_first(columns(n2, s1), d_up[...]),
        lambda s1: turn_first(columns(cot, s1), act[...]),
    )
    rets = [
        Return(at, sends, makers[i], room, refs.take(2), out_place(ffn_out[i]), refs.take(n_ret))
        for i, room in enumerate((gate_w, up_w, down_w))
    ]
    for ret, out in zip(rets, ffn_out):
        ret.short = nz * unit - out.shape[1]

    def summed(make, first, cols):
        room = wa.at[:, :, pl.ds(first, cols)]
        ret = Return(at, sends, make, room, refs.take(2), None, refs.take(n_ret))
        (land,) = refs.take(1)
        ret.chain = ChainSum(at, sends, (ret.piece, land), refs.take(n_sum))
        return ret

    r_qkv = summed(lambda s1: turn_first(columns(normed1_b, s1), d_projb[...]), 0, qkv_cols)
    r_out = summed(lambda s1: turn_first(columns(d_resid_b, s1), attn[...]), qkv_cols, q_cols)
    r_dn2, r_ffn = (
        Reduce(at, sends, parts, refs.take(3), refs.take(n_red)) for parts in (dn2_part, ffn_part)
    )
    (d_resid_f, d_attn, d_score, dkv, dkv_land, dn1_part, dn1_land, small_b, small_land, small_z,
     small_zland, small_y, small_yland, cosine, sine, mask, dkvs, dkvr, shs, shr, szs, szr, ysems,
     yrecv) = refs.take(24)

    at.greet(everyone=True)
    w_small.over_z()
    w_small.own_block()
    for item in (w_qkv, w_out):
        item.over_z()
        item.own_block()
    my_half = cot_in.at[pl.ds(pl.multiple_of(at.y * half, SUBLANES), half)]
    sends.here(cot_in.at[pl.ds(0, half)], cot.at[at.z, 0], cot_sem.at[0])
    sends.here(cot_in.at[pl.ds(half, half)], cot.at[at.z, 1], cot_sem.at[1])
    w_small.pass_z()
    w_qkv.pass_z()
    w_out.pass_z()
    ffn[0].over_z()
    ffn[1].over_z()
    for item in ffn:
        item.own_block()

    hidden_f = hidden[...].astype(F32)
    factor1 = lax.rsqrt(jnp.mean(hidden_f * hidden_f, axis=1, keepdims=True) + EPSILON)
    seg = segments[...].astype(F32)
    row = lax.broadcasted_iota(jnp.int32, (rows, group_rows), 0) + at.z * rows
    col = lax.broadcasted_iota(jnp.int32, (rows, group_rows), 1)
    seg_row = jnp.sum(jnp.where(row == col, seg, 0.0), axis=1, keepdims=True)
    earlier = jnp.sum(jnp.where(seg < seg_row, 1.0, 0.0), axis=1, keepdims=True)
    mask[...] = jnp.where((seg == seg_row) & (col <= row), 1.0, 0.0)
    position = row[:, :1].astype(F32) - earlier
    lane = lax.broadcasted_iota(jnp.int32, (1, HD), 1)
    pair = lax.rem(lane, HD // 2).astype(F32)
    angle = position * jnp.exp(pair * (-2.0 * math.log(THETA) / HD))
    cosine[...] = jnp.cos(angle)
    sine[...] = jnp.sin(angle) * jnp.where(lane < HD // 2, -1.0, 1.0)
    w_small.pass_s()
    w_qkv.pass_s()
    w_out.pass_s()
    w_small.finish()
    gains = whole_lines(small, ns * nz, depth)
    normed1_b[...] = (hidden[...].astype(F32) * factor1 * gains[0:1, :]).astype(BF16)
    width_each = HD // (ns * nz)
    lane = lax.broadcasted_iota(jnp.int32, (8, LANES), 1)
    bias = jnp.zeros((8, LANES), F32)
    for b in range(ns * nz):
        line = small[b, 8:16, :].astype(F32)
        moved = pltpu.roll(line, b * width_each, 1) if b else line
        bias = jnp.where((lane >= b * width_each) & (lane < (b + 1) * width_each), moved, bias)
    w_qkv.finish()
    cos_t, sin_t = cosine[...], sine[...]

    def projected(head):
        weight = wa[:, :, head * HD:(head + 1) * HD].reshape(width, HD)
        return jnp.dot(normed1_b[...], weight, preferred_element_type=F32) + bias[head:head + 1, :]

    def rotated(values):
        return values * cos_t + pltpu.roll(values, HD // 2, 1) * sin_t

    for j in range(kv):
        kv_all[at.z, :, j * HD:(j + 1) * HD] = rotated(projected(heads + j)).astype(BF16)
        kv_all[at.z, :, (kv + j) * HD:(kv + j + 1) * HD] = projected(heads + kv + j).astype(BF16)
    for there, z2 in at.near():
        sends.go(
            kv_all.at[at.z], kv_all.at[at.z], kvs.at[z2], kvr.at[at.z], only=there, context=z2
        )
    ffn[2].over_z()
    t_cot.over_z(my_half)
    for h in range(heads):
        query[:, h * HD:(h + 1) * HD] = rotated(projected(h)).astype(BF16)
    ffn[0].pass_z()
    ffn[1].pass_z()
    for d in range(1, nz):
        z1 = at.z_from(d)
        landed(kv_all.at[z1], kvs.at[z1], kvr.at[z1], context=z1)

    def keys_of(j):
        return kv_all[:, :, j * HD:(j + 1) * HD].reshape(group_rows, HD)

    keep = mask[...] > 0
    for h in range(heads):
        keys, values = keys_of(h // repeat), keys_of(kv + h // repeat)
        scores = turn_last(query[:, h * HD:(h + 1) * HD], keys)
        scores = jnp.where(keep, scores * scale, -1e30)
        peak = jnp.max(scores, axis=1, keepdims=True)
        lse = peak + jnp.log(jnp.sum(jnp.exp(scores - peak), axis=1, keepdims=True))
        p = jnp.exp(scores - lse)
        probs[h * rows:(h + 1) * rows, :] = p
        out = jnp.dot(p.astype(BF16), values, preferred_element_type=F32)
        attn[:, h * HD:(h + 1) * HD] = out.astype(BF16)
    w_out.finish()
    out_w = wa[:, :, qkv_cols:qkv_cols + q_cols].reshape(width, q_cols)
    part = turn_last(attn[...], out_w).astype(BF16)
    ypart[0] = part[:half]
    ypart[1] = part[half:]
    sends.go(ypart.at[at.twin], yland, yps, ypr, tensor=at.twin)
    ffn[0].pass_s()

    landed(yland, yps, ypr, tensor=at.twin)
    base = pl.multiple_of(at.y * half, SUBLANES)
    total = ypart[at.y].astype(F32) + yland[...].astype(F32)
    res = hidden[pl.ds(base, half), :].astype(F32) + total
    resid[...] = res
    factor2 = lax.rsqrt(jnp.mean(res * res, axis=1, keepdims=True) + EPSILON)
    n2[at.z, at.y] = (res * factor2 * gains[1:2, :]).astype(BF16)
    t_n2.over_z(n2.at[at.z, at.y])
    t_n2.over_y(at.z, n2.at[at.z, at.y])
    ffn[1].pass_s()
    ffn[2].pass_z()
    t_cot.pass_z()
    t_n2.pass_z([1])
    ffn[2].pass_s()
    t_cot.wait_y(range(nz), lambda z1: at.z != z1)
    for item in ffn:
        item.finish()
    for copy in sends.local:
        copy.wait()
    sends.local = []

    def weight(ref):
        return ref[...].reshape(width, -1)

    d_act[...] = jnp.dot(cot[...].reshape(group_rows, width), weight(down_w), preferred_element_type=F32)
    few, tall = nz // 2, 32
    chunk = few * rows

    def half_block(first):
        t_n2.wait_y([first * few + i for i in range(few)])
        start = pl.multiple_of(first * chunk, chunk)
        mine = n2[pl.ds(first * few, few)].reshape(chunk, width)
        gate[...] = jnp.dot(mine, weight(gate_w), preferred_element_type=F32)
        up_val[...] = jnp.dot(mine, weight(up_w), preferred_element_type=F32)

        @pl.loop(0, chunk // tall)
        def _(i):
            line = pl.ds(pl.multiple_of(i * tall, tall), tall)
            whole = pl.ds(pl.multiple_of(start + i * tall, tall), tall)
            g, u, d = gate[line, :], up_val[line, :], d_act[whole, :]
            sigma = jax.nn.sigmoid(g)
            silu_val = g * sigma
            act[whole, :] = (silu_val * u).astype(BF16)
            d_gate[whole, :] = (d * u * sigma * (1.0 + g * (1.0 - sigma))).astype(BF16)
            d_up[whole, :] = (d * silu_val).astype(BF16)

        span = pl.ds(start, chunk)
        dn2_part[pl.ds(first * few, few)] = (
            turn_last(d_gate[span, :], weight(gate_w)) + turn_last(d_up[span, :], weight(up_w))
        ).astype(BF16).reshape(few, 2, half, width)
        r_dn2.over_y([first * few + i for i in range(few)])

    nearer = lax.div(at.z, few)
    t_n2.pass_z(range(2, nz - 1))
    half_block(nearer)
    t_n2.pass_z([nz - 1])
    half_block(1 - nearer)
    w_sends.drain()

    rets[0].give_all()
    rets[0].over_s()
    r_dn2.pass_y(far_first(nz))
    rets[0].over_z(last=False)
    rets[1].give_all()
    rets[1].over_s()
    res = resid[...]
    factor2 = lax.rsqrt(jnp.mean(res * res, axis=1, keepdims=True) + EPSILON)
    unit2 = res * factor2
    dn2 = r_dn2.total()
    grad_g2 = jnp.sum(dn2 * unit2, axis=0, keepdims=True)
    scaled = dn2 * gains[1:2, :]
    back2 = factor2 * (scaled - unit2 * jnp.mean(scaled * unit2, axis=1, keepdims=True))
    d_res = cot[at.z, at.y].astype(F32) + back2
    d_resid_f[at.y] = d_res
    d_resid_b[at.y] = d_res.astype(BF16)
    mine_b, mine_f = d_resid_b.at[at.y], d_resid_f.at[at.y]
    sends.go(mine_b, mine_b, ysems.at[0], yrecv.at[0], tensor=at.twin)
    ffn_part[...] = turn_last(act[...], weight(down_w)).astype(BF16).reshape(nz, 2, half, width)
    rets[2].give_all()
    rets[2].over_s()
    landed(d_resid_b.at[at.twin], ysems.at[0], yrecv.at[0], tensor=at.twin)
    r_ffn.over_y(far_first(nz))
    sends.go(mine_f, mine_f, ysems.at[1], yrecv.at[1], tensor=at.twin)

    d_resid_all = d_resid_b[...].reshape(rows, width)
    out_w = wa[:, :, qkv_cols:qkv_cols + q_cols].reshape(width, q_cols)
    d_attn[...] = jnp.dot(d_resid_all, out_w, preferred_element_type=F32).astype(BF16)
    r_out.give_all()
    r_out.over_s()

    def unrotated(values):
        return values * cos_t - pltpu.roll(values, HD // 2, 1) * sin_t

    bias_rows = [None] * (heads + 2 * kv)

    def place(head, grad):
        bias_rows[head] = jnp.sum(grad, axis=0, keepdims=True)
        d_projb[:, head * HD:(head + 1) * HD] = grad.astype(BF16)

    for j in range(kv):
        keys, values = keys_of(j), keys_of(kv + j)
        d_values = jnp.zeros((group_rows, HD), F32)
        d_keys = jnp.zeros((group_rows, HD), F32)
        for h in range(j * repeat, (j + 1) * repeat):
            d_out = d_attn[:, h * HD:(h + 1) * HD]
            p = probs[h * rows:(h + 1) * rows, :]
            d_prob = turn_last(d_out, values)
            delta = jnp.sum(
                d_out.astype(F32) * attn[:, h * HD:(h + 1) * HD].astype(F32), axis=1, keepdims=True
            )
            d_score[...] = (p * (d_prob - delta)).astype(BF16)
            d_query = jnp.dot(d_score[...], keys, preferred_element_type=F32)
            place(h, unrotated(d_query * scale))
            d_keys = d_keys + turn_first(d_score[...], query[:, h * HD:(h + 1) * HD])
            d_values = d_values + turn_first(p.astype(BF16), d_out)
        for i, grad in ((j, d_keys * scale), (kv + j, d_values)):
            dkv[:, :, i * HD:(i + 1) * HD] = grad.astype(BF16).reshape(nz, rows, HD)
    for there, z2 in at.near():
        sends.go(dkv.at[z2], dkv_land.at[at.z], dkvs.at[z2], dkvr.at[at.z], only=there, context=z2)
    rets[0].over_z(first=False)
    rets[1].over_z(last=False)
    d_own = dkv[at.z].astype(F32)
    for d in range(1, nz):
        z1 = at.z_from(d)
        landed(dkv_land.at[z1], dkvs.at[z1], dkvr.at[z1], context=z1)
        d_own = d_own + dkv_land[z1].astype(F32)
    for j in range(kv):
        place(heads + j, unrotated(d_own[:, j * HD:(j + 1) * HD]))
        place(heads + kv + j, d_own[:, (kv + j) * HD:(kv + j + 1) * HD])
    qkv_w = wa[:, :, :qkv_cols].reshape(width, qkv_cols)
    dn1_part[...] = turn_last(d_projb[...], qkv_w).astype(BF16)
    sends.go(dn1_part, dn1_land, ysems.at[2], yrecv.at[2], tensor=at.twin)
    r_qkv.give_all()
    r_qkv.over_s()
    rets[1].over_z(first=False)
    r_ffn.pass_y(far_first(nz))
    rets[2].over_z(last=False)
    r_out.over_z()

    block_out[at.y] = (r_ffn.total() + resid[...]).astype(BF16)
    sends.go(block_out.at[at.y], block_out.at[at.y], ysems.at[3], yrecv.at[3], tensor=at.twin)

    landed(dn1_land, ysems.at[2], yrecv.at[2], tensor=at.twin)
    landed(d_resid_f.at[at.twin], ysems.at[1], yrecv.at[1], tensor=at.twin)
    dn1 = dn1_part[...].astype(F32) + dn1_land[...].astype(F32)
    hidden_f = hidden[...].astype(F32)
    factor1 = lax.rsqrt(jnp.mean(hidden_f * hidden_f, axis=1, keepdims=True) + EPSILON)
    unit1 = hidden_f * factor1
    row = lax.broadcasted_iota(jnp.int32, (rows, 1), 0)
    my_row = (row >= at.y * half) & (row < (at.y + 1) * half)
    grad_g1 = jnp.sum(jnp.where(my_row, dn1 * unit1, 0.0), axis=0, keepdims=True)
    scaled = dn1 * gains[0:1, :]
    back1 = factor1 * (scaled - unit1 * jnp.mean(scaled * unit1, axis=1, keepdims=True))
    input_grad[...] = d_resid_f[...].reshape(rows, width) + back1

    both = jnp.concatenate([grad_g1, grad_g2, jnp.zeros((6, width), F32)], axis=0)
    bias = jnp.concatenate(bias_rows, axis=0)
    for b in range(ns * nz):
        moved = pltpu.roll(bias, LANES - b * width_each, 1) if b else bias
        small_b[b // nz, b % nz] = jnp.concatenate([piece_of_lines(both, b, depth), moved], axis=0)
    for k in range(1, ns):
        s2 = lax.rem(at.s + k, ns)
        sends.go(small_b.at[s2], small_land.at[k], shs.at[k], shr.at[k], shard=s2)
    rets[2].over_z(first=False)
    total = small_b[at.s]
    for k in range(1, ns):
        s1 = lax.rem(at.s - k + ns, ns)
        landed(small_land.at[k], shs.at[k], shr.at[k], shard=s1)
        total = total + small_land[k]
    small_z[...] = total
    for d in range(1, nz):
        sends.go(small_z.at[at.z_to(d)], small_zland.at[d], szs.at[d], szr.at[d], context=at.z_to(d))
    r_qkv.over_z()
    total = small_z[at.z]
    for d in range(1, nz):
        landed(small_zland.at[d], szs.at[d], szr.at[d], context=at.z_from(d))
        total = total + small_zland[d]
    small_y[...] = total
    sends.go(small_y, small_yland, ysems.at[4], yrecv.at[4], tensor=at.twin)
    out_grad[...] = r_out.chain.total(r_out.piece(at.z)[...].astype(F32))
    qkv_grad[...] = r_qkv.chain.total(r_qkv.piece(at.z)[...].astype(F32))
    landed(small_yland, ysems.at[4], yrecv.at[4], tensor=at.twin)
    small_out[:8, :] = small_y[:8, :] + small_yland[:8, :]
    small_out[8:, :] = small_y[8:, :]
    landed(block_out.at[at.twin], ysems.at[3], yrecv.at[3], tensor=at.twin)
    for ret in rets:
        ret.finish()
    sends.drain()


def layer(ns, nz, heads, kv, hidden_units, qkv_in, out_in, small_in, ffn_in, hidden, cot, segments):
    rows, width = hidden.shape
    owners, half, group_rows = ns * nz, rows // 2, nz * rows
    depth, cols = qkv_in.shape[0], qkv_in.shape[1] + out_in.shape[1]
    unit = ffn_in[0].shape[2]
    q_cols, kv_cols = heads * HD, 2 * kv * HD
    qkv_cols = q_cols + kv_cols
    dma = pltpu.SemaphoreType.DMA
    shape = jax.ShapeDtypeStruct
    room = pltpu.VMEM
    vmem = pl.BlockSpec(memory_space=pltpu.VMEM)
    anyspace = pl.BlockSpec(memory_space=pl.ANY)
    scratch = [room((ns, nz * depth, cols), BF16)] + [room((ns, nz * depth, unit), BF16)] * 3
    scratch += [
        room((owners, 16, LANES), BF16),
        room((2, half, width), BF16),
        room((half, width), BF16),
        room((nz, 2, half, width), BF16),
        room((nz, 2, half, width), BF16),
        room((half, width), F32),
        room((rows, q_cols), BF16),
        room((nz, rows, kv_cols), BF16),
        room((heads * rows, group_rows), F32),
        room((rows, q_cols), BF16),
    ]
    scratch += Spread.sems(ns, nz) * 6 + Tokens.sems(nz) * 2
    scratch += [dma((nz,)), dma((nz,)), dma, dma, dma((2,))]
    scratch += [room((group_rows // 2, unit), F32)] * 2 + [room((group_rows, unit), F32)]
    scratch += [room((group_rows, unit), BF16)] * 3 + [room((nz, 2, half, width), BF16)] * 2
    scratch += [
        room((rows, width), BF16), room((2, half, width), BF16), room((rows, qkv_cols), BF16),
    ]
    for _ in range(3):
        scratch += Return.lands(ns, nz, depth, unit) + Return.sems(ns, nz)
    for n in (qkv_cols, q_cols):
        scratch += Return.lands(ns, nz, depth, n) + Return.sems(ns, nz)
        scratch += ChainSum.bufs(nz, (depth, n))[1:] + ChainSum.sems(nz)
    for _ in range(2):
        scratch += Reduce.bufs(nz, half, width) + Reduce.sems(nz)
    scratch += [
        room((2, half, width), F32),
        room((rows, q_cols), BF16),
        room((rows, group_rows), BF16),
        room((nz, rows, kv_cols), BF16),
        room((nz, rows, kv_cols), BF16),
        room((rows, width), BF16),
        room((rows, width), BF16),
        room((ns, nz, 16, LANES), F32),
        room((ns, nz, 16, LANES), F32),
        room((nz, 16, LANES), F32),
        room((nz, 16, LANES), F32),
        room((16, LANES), F32),
        room((16, LANES), F32),
        room((rows, HD), F32),
        room((rows, HD), F32),
        room((rows, group_rows), F32),
        dma((nz,)), dma((nz,)), dma((ns,)), dma((ns,)), dma((nz,)), dma((nz,)), dma((5,)), dma((5,)),
    ]
    return pl.pallas_call(
        functools.partial(layer_kernel, ns, nz, heads, kv),
        out_shape=[
            shape((2, half, width), BF16),
            shape((rows, width), F32),
            shape((depth, qkv_cols), F32),
            shape((depth, q_cols), F32),
            shape((16, LANES), F32),
            *[shape((depth, hidden_units), BF16)] * 3,
        ],
        in_specs=[anyspace] * 6 + [vmem, anyspace, vmem],
        out_specs=[vmem] * 5 + [anyspace] * 3,
        scratch_shapes=scratch,
        compiler_params=pltpu.CompilerParams(
            collective_id=0, has_side_effects=True, vmem_limit_bytes=VMEM_BYTES
        ),
    )(qkv_in, out_in, small_in, *ffn_in, hidden, cot, segments)


def fast_step(
    ns,
    nz,
    hidden_in,
    segment_ids,
    attn_gain,
    qkv_weight,
    qkv_bias,
    out_weight,
    ffn_gain,
    gate_weight,
    up_weight,
    down_weight,
    out_cotangent,
):
    rows, width = hidden_in.shape
    depth, hidden_units = gate_weight.shape
    parts = 2
    heads = H // parts
    kv = KVH // parts
    unit_cols = -(-hidden_units // (nz * LANES)) * LANES
    padded = unit_cols * nz

    def by_place(weight):
        full = jnp.pad(weight, ((0, 0), (0, padded - hidden_units)))
        return jnp.transpose(full.reshape(depth, nz, unit_cols), (1, 0, 2))

    ffn_in = [by_place(w) for w in (gate_weight, up_weight, down_weight.T)]
    gains_in = jnp.pad(jnp.stack([attn_gain, ffn_gain]), ((0, 6), (0, LANES - depth)))
    bias_in = jnp.pad(qkv_bias, ((0, 0), (0, LANES - qkv_bias.shape[1])))
    small_in = jnp.concatenate([gains_in, bias_in], axis=0)

    block_out, input_grad, grad_qkv, grad_out, small, grad_gate, grad_up, grad_down = layer(
        ns, nz, heads, kv, hidden_units, qkv_weight, out_weight.T, small_in, ffn_in, hidden_in,
        out_cotangent, segment_ids,
    )

    return (
        block_out.reshape(rows, width),
        input_grad,
        small[0, :depth],
        grad_qkv,
        small[8:, : qkv_bias.shape[1]],
        grad_out.T,
        small[1, :depth],
        grad_gate.astype(F32),
        grad_up.astype(F32),
        grad_down.astype(F32).T,
    )


def general_step(
    hidden_in,
    segment_ids,
    attn_gain,
    qkv_weight,
    qkv_bias,
    out_weight,
    ffn_gain,
    gate_weight,
    up_weight,
    down_weight,
    out_cotangent,
):
    rows, width = hidden_in.shape
    depth = gate_weight.shape[0]
    hidden_units = gate_weight.shape[1]
    parts = lax.axis_size("tensor")
    blocks = lax.axis_size("context")
    heads = H // parts
    kv = KVH // parts
    repeat = H // KVH
    scale = HD ** (-0.5)
    block_index = lax.axis_index("context")
    part_index = lax.axis_index("tensor")
    half_rows = rows // parts
    unit_cols = -(-hidden_units // (blocks * LANES)) * LANES
    padded = unit_cols * blocks

    def spread(weight):
        full = jnp.pad(weight, ((0, 0), (0, padded - hidden_units)))
        mine = lax.all_to_all(full, "context", split_axis=1, concat_axis=0, tiled=True)
        mine = mine.reshape(blocks * depth, unit_cols)
        return lax.all_gather(mine, "shard", axis=0, tiled=True)

    gate_full = spread(gate_weight)
    up_full = spread(up_weight)
    down_full = spread(down_weight.T)
    gain_one = lax.all_gather(attn_gain, OWNERS, axis=0, tiled=True).astype(F32)
    gain_two = lax.all_gather(ffn_gain, OWNERS, axis=0, tiled=True).astype(F32)
    bias = lax.all_gather(qkv_bias, OWNERS, axis=1, tiled=True).reshape(-1).astype(F32)
    qkv_full = lax.all_gather(qkv_weight, OWNERS, axis=0, tiled=True)
    out_full = lax.all_gather(out_weight.T, OWNERS, axis=0, tiled=True)

    seg_all = segment_ids[0]
    group_rows = seg_all.shape[0]
    first_row = block_index * rows
    index_all = jnp.arange(group_rows, dtype=jnp.int32)
    earlier = jnp.sum((seg_all[None, :] < seg_all[:, None]).astype(jnp.int32), axis=1)
    positions = index_all - earlier
    seg_local = lax.dynamic_slice_in_dim(seg_all, first_row, rows)
    index_local = first_row + jnp.arange(rows, dtype=jnp.int32)
    allowed = (seg_local[:, None] == seg_all[None, :]) & (
        index_local[:, None] >= index_all[None, :]
    )
    cosine, sine = rotary_tables(positions)
    cos_local = lax.dynamic_slice_in_dim(cosine, first_row, rows)
    sin_local = lax.dynamic_slice_in_dim(sine, first_row, rows)

    hidden_all = lax.all_gather(hidden_in, "context", axis=0, tiled=True)
    normed_all, _, _ = norm_forward(hidden_all.astype(F32), gain_one)
    hidden_f = hidden_in.astype(F32)
    normed1, unit1, factor1 = norm_forward(hidden_f, gain_one)
    q_cols = heads * HD
    k_cols = kv * HD
    query_f = dot(normed1, qkv_full[:, :q_cols]) + bias[:q_cols]
    kv_f = dot(normed_all, qkv_full[:, q_cols:]) + bias[q_cols:]
    query = jnp.transpose(query_f.reshape(rows, heads, HD), (1, 0, 2))
    query = rotate(query, cos_local, sin_local).astype(BF16)
    keys = jnp.transpose(kv_f[:, :k_cols].reshape(group_rows, kv, HD), (1, 0, 2))
    keys = rotate(keys, cosine, sine).astype(BF16)
    values = jnp.transpose(kv_f[:, k_cols:].reshape(group_rows, kv, HD), (1, 0, 2)).astype(BF16)
    query = query.reshape(kv, repeat * rows, HD)
    mask = jnp.tile(allowed, (repeat, 1))
    scores = jnp.where(mask, batched(query, keys, 2, 2) * scale, -1e30)
    peak = jnp.max(scores, axis=2, keepdims=True)
    lse = peak + jnp.log(jnp.sum(jnp.exp(scores - peak), axis=2, keepdims=True))
    p_soft = jnp.exp(scores - lse)
    probs = p_soft.astype(BF16)
    outs = batched(probs, values, 2, 1).astype(BF16)
    attn = jnp.transpose(outs.reshape(heads, rows, HD), (1, 0, 2)).reshape(rows, q_cols)
    attn_part = contract_last(attn, out_full).astype(BF16)

    mine = part_index * half_rows
    attn_half = lax.psum_scatter(attn_part, "tensor", scatter_dimension=0, tiled=True)
    resid_half = lax.dynamic_slice_in_dim(hidden_f, mine, half_rows) + attn_half.astype(F32)
    normed2_half, unit2, factor2 = norm_forward(resid_half, gain_two)
    normed2 = lax.all_gather(normed2_half, TEAM, axis=0, tiled=True)
    cot_half = lax.dynamic_slice_in_dim(out_cotangent, mine, half_rows)
    cot = lax.all_gather(cot_half, TEAM, axis=0, tiled=True)

    gate = dot(normed2, gate_full)
    up_val = dot(normed2, up_full)
    sigma = jax.nn.sigmoid(gate)
    silu_val = gate * sigma
    act = (silu_val * up_val).astype(BF16)
    ffn_part = contract_last(act, down_full).astype(BF16)
    d_act = dot(cot, down_full)
    d_gate = (d_act * up_val * sigma * (1.0 + gate * (1.0 - sigma))).astype(BF16)
    d_up = (d_act * silu_val).astype(BF16)
    dn2_part = (contract_last(d_gate, gate_full) + contract_last(d_up, up_full)).astype(BF16)
    ffn_half = lax.psum_scatter(ffn_part, TEAM, scatter_dimension=0, tiled=True)
    block_half = (resid_half + ffn_half.astype(F32)).astype(BF16)
    block_out = lax.all_gather(block_half, "tensor", axis=0, tiled=True)
    dn2_half = lax.psum_scatter(dn2_part, TEAM, scatter_dimension=0, tiled=True).astype(F32)
    grad_g2, d_back2 = norm_backward(dn2_half, unit2, factor2, gain_two)
    d_resid_half = cot_half.astype(F32) + d_back2

    def give_back(grad):
        part = lax.psum_scatter(grad.astype(BF16), "shard", scatter_dimension=0, tiled=True)
        part = part.reshape(blocks, depth, unit_cols)
        part = lax.all_to_all(part, "context", split_axis=0, concat_axis=2, tiled=True)
        return part.reshape(depth, padded)[:, :hidden_units].astype(F32)

    sum_gate = give_back(contract_first(normed2, d_gate))
    sum_up = give_back(contract_first(normed2, d_up))
    sum_down = give_back(contract_first(cot, act)).T

    d_resid_b = lax.all_gather(d_resid_half.astype(BF16), "tensor", axis=0, tiled=True)
    grad_out = contract_first(d_resid_b, attn)
    d_attn = dot(d_resid_b, out_full).astype(BF16)
    d_outs = jnp.transpose(d_attn.reshape(rows, heads, HD), (1, 0, 2)).reshape(
        kv, repeat * rows, HD
    )
    d_prob = batched(d_outs, values, 2, 2)
    delta = jnp.sum(d_outs.astype(F32) * outs.astype(F32), axis=2, keepdims=True)
    d_score = (p_soft * (d_prob - delta)).astype(BF16)
    d_query = batched(d_score, keys, 2, 1) * scale
    d_keys = batched(d_score, query, 1, 1) * scale
    d_values = batched(probs, d_outs, 1, 1)
    d_kv = jnp.concatenate([d_keys, d_values], axis=0).astype(BF16)
    d_kv = lax.psum_scatter(d_kv, "context", scatter_dimension=1, tiled=True).astype(F32)
    d_query = unrotate(d_query.reshape(heads, rows, HD), cos_local, sin_local)
    d_keys = unrotate(d_kv[:kv], cos_local, sin_local)
    d_proj = jnp.transpose(jnp.concatenate([d_query, d_keys, d_kv[kv:]], axis=0), (1, 0, 2))
    grad_bias = jnp.sum(d_proj, axis=0)
    d_projb = d_proj.reshape(rows, -1).astype(BF16)
    grad_qkv = contract_first(normed1, d_projb)
    dn1_part = contract_last(d_projb, qkv_full).astype(BF16)
    dn1_half = lax.psum_scatter(dn1_part, "tensor", scatter_dimension=0, tiled=True).astype(F32)
    unit1_half = lax.dynamic_slice_in_dim(unit1, mine, half_rows)
    factor1_half = lax.dynamic_slice_in_dim(factor1, mine, half_rows)
    grad_g1, d_back1 = norm_backward(dn1_half, unit1_half, factor1_half, gain_one)
    input_grad = lax.all_gather(d_resid_half + d_back1, "tensor", axis=0, tiled=True)

    gains = lax.psum(jnp.stack([grad_g1, grad_g2]), "tensor")
    sum_gains = lax.psum_scatter(gains, OWNERS, scatter_dimension=1, tiled=True)
    sum_qkv = lax.psum_scatter(grad_qkv.astype(BF16), OWNERS, scatter_dimension=0, tiled=True)
    sum_bias = lax.psum_scatter(grad_bias, OWNERS, scatter_dimension=1, tiled=True)
    sum_out = lax.psum_scatter(grad_out.astype(BF16), OWNERS, scatter_dimension=0, tiled=True)
    return (
        block_out,
        input_grad,
        sum_gains[0],
        sum_qkv.astype(F32),
        sum_bias,
        sum_out.astype(F32).T,
        sum_gains[1],
        sum_gate,
        sum_up,
        sum_down,
    )


def solution(mesh):
    ns, nz, parts = (mesh.shape[a] for a in ("shard", "context", "tensor"))
    rows = P(OWNERS, None)

    def local(*args):
        depth = args[7].shape[0]
        if depth % SUBLANES == 0 and ns % 2 == 0 and ns > 2 and nz % 2 == 0 and parts == 2:
            return fast_step(ns, nz, *args)
        return general_step(*args)

    placed = (
        rows,
        P("shard", None),
        P(OWNERS),
        P(OWNERS, "tensor"),
        P("tensor", OWNERS),
        P("tensor", OWNERS),
        P(OWNERS),
        P(OWNERS, "tensor"),
        P(OWNERS, "tensor"),
        P("tensor", OWNERS),
        rows,
    )
    return jax.shard_map(
        local,
        mesh=mesh,
        in_specs=placed,
        out_specs=(
            rows,
            rows,
            P(OWNERS),
            P(OWNERS, "tensor"),
            P("tensor", OWNERS),
            P("tensor", OWNERS),
            P(OWNERS),
            P(OWNERS, "tensor"),
            P(OWNERS, "tensor"),
            P("tensor", OWNERS),
        ),
        check_vma=False,
    )
```

profile of v0, /device:TPU:10, one launch (start us, length us, event | category | flops | bytes accessed | tf_op | source)
XLA Modules:
  0.0 298.7 jit_solution(3083554534594303314)
XLA Ops:
  0.6 0.7 fusion.7
  1.3 1.3 fusion.1.refs_2_
  2.6 0.0 copy-start.2
  2.6 1.3 pad.20
  3.9 0.0 copy-start.3
  3.9 1.0 copy.30
  4.9 0.0 copy-done.2
  4.9 0.1 pad.21
  5.0 0.4 copy-done.3
  5.4 0.1 pad.22
  5.5 1.3 bitcast_bitcast_fusion
  6.8 281.0 %shard_map.186 = (bf16[2,64,1536]{2,1,0:T(8,128)(2,1)}, f32[128,1536]{1,0:T(8,128)}, f32[96,1024]{1,0:T(8,128)}, f32[96,768]{1,0:T(8,128)}, f32[16,128]{1,0:T(8,...) custom-call(bf16[96,1024]{1,0:T(8,128)(2,1)} %refs_0_.1, ...), custom_call_target="tpu_custom_call" | custom-call | tf_op jit(solution)/shard_map/pallas_call | solution.py:1014
  287.8 0.0 copy-start.1
  287.8 1.3 slice_bitcast_fusion
  289.1 1.3 slice.10
  290.4 2.5 convert_element_type.15
  292.8 0.0 copy-done.1
  292.8 0.0 copy-start
  292.8 1.3 convert_element_type.16
  294.1 0.2 copy-done
  294.3 0.0 copy-start.6
  294.3 0.0 copy-start.4
  294.3 1.3 convert_bitcast_fusion
  295.6 0.0 copy-done.6
  295.6 0.0 copy-start.5
  295.6 0.0 copy-start.7
  295.6 0.7 copy.35
  296.4 0.0 copy-done.4
  296.4 0.9 copy.36
  297.3 0.0 copy-done.5
  297.3 0.7 copy.37
  298.0 0.0 copy-done.7
  298.0 0.7 copy.38
Async XLA Ops:
  2.6 2.3 copy-start.2
  3.9 1.5 copy-start.3
  287.8 5.0 %copy-start.1 = (bf16[96,4480]{1,0:T(8,128)(2,1)S(1)}, bf16[96,4480]{1,0:T(8,128)(2,1)}, u32[]{:S(2)}) copy-start(bf16[96,4480]{1,0:T(8,128)(2,1)} %get-tuple-element.24) | copy-start | bytes 2580484
  292.8 1.5 copy-start
  294.3 1.3 copy-start.6
  294.3 2.1 copy-start.4
  295.6 1.6 copy-start.5
  295.6 2.4 copy-start.7
where the time goes:
time: 301 us; the launch traced here: 299 us
  Pallas kernels  281 us (93%)
  local copies, waits for them, and re-layouts  10 us (3%)
  other arithmetic  7.03 us (2%)
    pallas_call x1, Pallas kernels, layer(): pl.pallas_call(functools.partial(layer_kernel, ns, nz, heads, kv), out_sh...  281 us

commit v1 on v0

--- a/solution.py
+++ b/solution.py
@@ -679,16 +679,6 @@
     my_half = cot_in.at[pl.ds(pl.multiple_of(at.y * half, SUBLANES), half)]
     sends.here(cot_in.at[pl.ds(0, half)], cot.at[at.z, 0], cot_sem.at[0])
     sends.here(cot_in.at[pl.ds(half, half)], cot.at[at.z, 1], cot_sem.at[1])
-    w_small.pass_z()
-    w_qkv.pass_z()
-    w_out.pass_z()
-    ffn[0].over_z()
-    ffn[1].over_z()
-    for item in ffn:
-        item.own_block()
-
-    hidden_f = hidden[...].astype(F32)
-    factor1 = lax.rsqrt(jnp.mean(hidden_f * hidden_f, axis=1, keepdims=True) + EPSILON)
     seg = segments[...].astype(F32)
     row = lax.broadcasted_iota(jnp.int32, (rows, group_rows), 0) + at.z * rows
     col = lax.broadcasted_iota(jnp.int32, (rows, group_rows), 1)
@@ -701,6 +691,16 @@
     angle = position * jnp.exp(pair * (-2.0 * math.log(THETA) / HD))
     cosine[...] = jnp.cos(angle)
     sine[...] = jnp.sin(angle) * jnp.where(lane < HD // 2, -1.0, 1.0)
+    for k in range(1, nz):
+        for item in (w_small, w_qkv, w_out):
+            item.pass_z([k])
+    ffn[0].over_z()
+    ffn[1].over_z()
+    for item in ffn:
+        item.own_block()
+
+    hidden_f = hidden[...].astype(F32)
+    factor1 = lax.rsqrt(jnp.mean(hidden_f * hidden_f, axis=1, keepdims=True) + EPSILON)
     w_small.pass_s()
     w_qkv.pass_s()
     w_out.pass_s()
@@ -843,6 +843,7 @@
     ffn_part[...] = turn_last(act[...], weight(down_w)).astype(BF16).reshape(nz, 2, half, width)
     rets[2].give_all()
     rets[2].over_s()
+    rets[0].over_z(first=False)
     landed(d_resid_b.at[at.twin], ysems.at[0], yrecv.at[0], tensor=at.twin)
     r_ffn.over_y(far_first(nz))
     sends.go(mine_f, mine_f, ysems.at[1], yrecv.at[1], tensor=at.twin)
@@ -882,7 +883,6 @@
             dkv[:, :, i * HD:(i + 1) * HD] = grad.astype(BF16).reshape(nz, rows, HD)
     for there, z2 in at.near():
         sends.go(dkv.at[z2], dkv_land.at[at.z], dkvs.at[z2], dkvr.at[at.z], only=there, context=z2)
-    rets[0].over_z(first=False)
     rets[1].over_z(last=False)
     d_own = dkv[at.z].astype(F32)
     for d in range(1, nz):

time: 301 us -> 296 us (0.983)
  Pallas kernels: 281 us -> 274 us
    pallas_call x1, Pallas kernels: 281 us -> 274 us  [layer(): pl.pallas_call(functools.partial(layer_kernel, ns, nz, heads, kv), out_sh...]
where the time goes in v1:
time: 296 us; the launch traced here: 292 us
  Pallas kernels  274 us (93%)
  local copies, waits for them, and re-layouts  10 us (3%)
  other arithmetic  7.03 us (2%)
    pallas_call x1, Pallas kernels, layer(): pl.pallas_call(functools.partial(layer_kernel, ns, nz, heads, kv), out_sh...  274 us

profile of v1, /device:TPU:10, one launch (start us, length us, event | category | flops | bytes accessed | tf_op | source)
XLA Modules:
  0.0 291.6 jit_solution(14921005918080055934)
XLA Ops:
  0.6 0.7 fusion.7
  1.3 1.3 fusion.1.refs_2_
  2.6 0.0 copy-start.2
  2.6 1.3 pad.20
  3.9 0.0 copy-start.3
  3.9 1.0 copy.30
  4.9 0.0 copy-done.2
  4.9 0.1 pad.21
  5.0 0.4 copy-done.3
  5.4 0.1 pad.22
  5.5 1.3 bitcast_bitcast_fusion
  6.8 273.9 %shard_map.186 = (bf16[2,64,1536]{2,1,0:T(8,128)(2,1)}, f32[128,1536]{1,0:T(8,128)}, f32[96,1024]{1,0:T(8,128)}, f32[96,768]{1,0:T(8,128)}, f32[16,128]{1,0:T(8,...) custom-call(bf16[96,1024]{1,0:T(8,128)(2,1)} %refs_0_.1, ...), custom_call_target="tpu_custom_call" | custom-call | tf_op jit(solution)/shard_map/pallas_call | solution.py:1014
  280.7 0.0 copy-start.1
  280.7 1.3 slice_bitcast_fusion
  282.0 1.3 slice.10
  283.3 2.5 convert_element_type.15
  285.7 0.0 copy-done.1
  285.7 0.0 copy-start
  285.7 1.3 convert_element_type.16
  287.0 0.2 copy-done
  287.2 0.0 copy-start.6
  287.2 0.0 copy-start.4
  287.2 1.3 convert_bitcast_fusion
  288.5 0.0 copy-done.6
  288.5 0.0 copy-start.5
  288.5 0.0 copy-start.7
  288.5 0.7 copy.35
  289.3 0.0 copy-done.4
  289.3 0.9 copy.36
  290.1 0.0 copy-done.5
  290.1 0.7 copy.37
  290.9 0.0 copy-done.7
  290.9 0.7 copy.38
Async XLA Ops:
  2.6 2.3 copy-start.2
  3.9 1.5 copy-start.3
  280.7 5.0 %copy-start.1 = (bf16[96,4480]{1,0:T(8,128)(2,1)S(1)}, bf16[96,4480]{1,0:T(8,128)(2,1)}, u32[]{:S(2)}) copy-start(bf16[96,4480]{1,0:T(8,128)(2,1)} %get-tuple-element.24) | copy-start | bytes 2580484
  285.7 1.5 copy-start
  287.2 1.3 copy-start.6
  287.2 2.1 copy-start.4
  288.5 1.6 copy-start.5
  288.5 2.4 copy-start.7
